TPU v7x, 32 devices: a whole 2x2x4 slice. The times are simulated.
32 devices in a mesh: fsdp: 8 (over z, x), dp: 4 (over y, core).
Axes of the slice: x: 2, y: 2, z: 4, core: 2. Of those that a mesh axis runs over, the one named last changes fastest.
Arguments:
- inputs: bfloat16 [32768, 768], P(('fsdp', 'dp')), may hold values from -6 to 6
- row_ids: int32 [32768], P(('fsdp', 'dp')), may hold values from 0 to 7, as said below
- ln_gains: bfloat16 [2, 768], P(None, 'fsdp'), may hold values from 0.099609375 to 1.8984375
- biases: bfloat16 [6, 768], P(None, 'fsdp'), may hold values from -3 to 3
- w_qkv: bfloat16 [768, 2304], P('fsdp'), may hold values from -0.21875 to 0.21875
- w_out: bfloat16 [768, 768], P('fsdp'), may hold values from -0.75 to 0.75
- w_up: bfloat16 [768, 3072], P('fsdp'), may hold values from -0.21875 to 0.21875
- bias_up: bfloat16 [3072], P('fsdp'), may hold values from -3 to 3
- w_down: bfloat16 [3072, 768], P('fsdp'), may hold values from -0.109375 to 0.109375
- cotangent: bfloat16 [32768, 768], P(('fsdp', 'dp')), may hold values from -6 to 6
Outputs:
- block_out: bfloat16 [32768, 768], P(('fsdp', 'dp'))
- d_inputs: float32 [32768, 768], P(('fsdp', 'dp'))
- g_ln_gains: float32 [2, 768], P(None, 'fsdp')
- g_biases: float32 [6, 768], P(None, 'fsdp')
- g_w_qkv: float32 [768, 2304], P('fsdp')
- g_w_out: float32 [768, 768], P('fsdp')
- g_w_up: float32 [768, 3072], P('fsdp')
- g_bias_up: float32 [3072], P('fsdp')
- g_w_down: float32 [3072, 768], P('fsdp')
Inputs may be any that keep to these rules, and one draw needn't show every extreme that they name: `row_ids`: on each device the 1024 tokens form rows of 128 or 256 consecutive tokens, the longer rows first, so that each row starts at a multiple of its own length; the value numbers a token's row on its device from 0 in order; some device holds only rows of 128.
All inputs are finite; a program needn't handle non-finite values.
Results may differ from a plain program's by a relative error of at most 0.011.
Values may be sent and summed in bfloat16 or wider, within the bound.
A program may use at most 256 MiB of HBM per device.

v0:
```python
import math
import jax
import jax.numpy as jnp
from jax import lax
from jax.sharding import PartitionSpec as P

HEADS = 12
HEAD = 64
BLOCK = 512
norm_eps = 1e-05


def layer_norm(values, gain, shift):
    center = values - jnp.mean(values, axis=-1, keepdims=True)
    spread = jnp.mean(center * center, axis=-1, keepdims=True)
    return center * lax.rsqrt(spread + norm_eps) * gain + shift


def gelu_tanh(values):
    inner = math.sqrt(2.0 / math.pi) * (values + 0.044715 * values * values * values)
    return 0.5 * values * (1.0 + jnp.tanh(inner))


def contract_rows(left, right):
    return lax.dot_general(
        left, right, (((0,), (0,)), ((), ())), preferred_element_type=jnp.float32
    )


def contract_cols(left, right):
    return lax.dot_general(
        left, right, (((1,), (1,)), ((), ())), preferred_element_type=jnp.float32
    )


def split_heads(values):
    return values.reshape(values.shape[0], HEADS, values.shape[1] // HEADS)


def block_scores(query, keys, query_rows, key_rows):
    raw_scores = jnp.einsum(
        "qhd,khd->hqk", split_heads(query), split_heads(keys), preferred_element_type=jnp.float32
    )
    raw_scores = raw_scores * (1.0 / math.sqrt(HEAD))
    same_row = (query_rows[:, None] == key_rows[None, :])[None]
    return jnp.where(same_row, raw_scores, -1000000000.0)


def attend_forward(query, keys, values, query_rows, key_rows):
    scores = block_scores(query, keys, query_rows, key_rows)
    row_max = jnp.max(scores, axis=-1, keepdims=True)
    exponent = jnp.exp(scores - row_max)
    row_sum = jnp.sum(exponent, axis=-1, keepdims=True)
    attn_probs = (exponent / row_sum).astype(jnp.bfloat16)
    result = jnp.einsum(
        "hqk,khd->qhd", attn_probs, split_heads(values), preferred_element_type=jnp.float32
    )
    return (result.reshape(query.shape[0], -1), (row_max + jnp.log(row_sum))[..., 0])


def attend_backward(query, keys, values, query_rows, key_rows, log_sums, grad_out):
    scores = block_scores(query, keys, query_rows, key_rows)
    attn_probs = jnp.exp(scores - log_sums[..., None])
    probs_low = attn_probs.astype(jnp.bfloat16)
    grad_heads = split_heads(grad_out)
    d_values = jnp.einsum("hqk,qhd->khd", probs_low, grad_heads, preferred_element_type=jnp.float32)
    d_probs = jnp.einsum(
        "qhd,khd->hqk", grad_heads, split_heads(values), preferred_element_type=jnp.float32
    )
    inner = jnp.sum(attn_probs * d_probs, axis=-1, keepdims=True)
    d_scores = (attn_probs * (d_probs - inner)).astype(jnp.bfloat16)
    scale = 1.0 / math.sqrt(HEAD)
    d_query = (
        jnp.einsum("hqk,khd->qhd", d_scores, split_heads(keys), preferred_element_type=jnp.float32)
        * scale
    )
    d_keys = (
        jnp.einsum("hqk,qhd->khd", d_scores, split_heads(query), preferred_element_type=jnp.float32)
        * scale
    )
    return (
        d_query.reshape(query.shape[0], -1),
        d_keys.reshape(keys.shape[0], -1),
        d_values.reshape(keys.shape[0], -1),
    )


def per_device(inputs, row_ids, ln_gains, biases, w_qkv, w_out, w_up, bias_up, w_down, cotangent):
    gathered = (
        lax.all_gather(ln_gains, "fsdp", axis=1, tiled=True),
        lax.all_gather(biases, "fsdp", axis=1, tiled=True),
        lax.all_gather(w_qkv, "fsdp", axis=0, tiled=True),
        lax.all_gather(w_out, "fsdp", axis=0, tiled=True),
        lax.all_gather(w_up, "fsdp", axis=0, tiled=True),
        lax.all_gather(bias_up, "fsdp", axis=0, tiled=True),
        lax.all_gather(w_down, "fsdp", axis=0, tiled=True),
    )
    gains = gathered[0].astype(jnp.float32)
    shifts = gathered[1].astype(jnp.float32)
    full_qkv, full_out, full_up, full_bias_up, full_down = (
        gathered[2],
        gathered[3],
        gathered[4],
        gathered[5],
        gathered[6],
    )
    width = full_out.shape[0]
    rows_n = inputs.shape[0]
    blocks_n = rows_n // BLOCK
    tokens_f = inputs.astype(jnp.float32)
    normed_f, norm_pull = jax.vjp(layer_norm, tokens_f, gains[0], shifts[0])
    normed = normed_f.astype(jnp.bfloat16)
    qkv_bias = jnp.concatenate([shifts[1], jnp.zeros_like(shifts[1]), shifts[2]])
    qkv = (jnp.dot(normed, full_qkv, preferred_element_type=jnp.float32) + qkv_bias).astype(
        jnp.bfloat16
    )
    query = qkv[:, :width]
    keys = qkv[:, width : 2 * width]
    values = qkv[:, 2 * width :]
    query_blocks = query.reshape(blocks_n, BLOCK, width)
    row_blocks = row_ids.reshape(blocks_n, BLOCK)

    def forward_block(entry):
        return attend_forward(entry[0], keys, values, entry[1], row_ids)

    mixed, log_sums = lax.map(forward_block, (query_blocks, row_blocks))
    mixed = mixed.reshape(rows_n, width).astype(jnp.bfloat16)
    middle = tokens_f + jnp.dot(mixed, full_out, preferred_element_type=jnp.float32) + shifts[3]
    normed_two_f, second_pull = jax.vjp(layer_norm, middle, gains[1], shifts[4])
    normed_two = normed_two_f.astype(jnp.bfloat16)
    upper = jnp.dot(normed_two, full_up, preferred_element_type=jnp.float32) + full_bias_up.astype(
        jnp.float32
    )
    hidden_f, gelu_pull = jax.vjp(gelu_tanh, upper)
    hidden = hidden_f.astype(jnp.bfloat16)
    block_out = (
        middle + jnp.dot(hidden, full_down, preferred_element_type=jnp.float32) + shifts[5]
    ).astype(jnp.bfloat16)
    again = (
        lax.all_gather(ln_gains, "fsdp", axis=1, tiled=True),
        lax.all_gather(biases, "fsdp", axis=1, tiled=True),
        lax.all_gather(w_qkv, "fsdp", axis=0, tiled=True),
        lax.all_gather(w_out, "fsdp", axis=0, tiled=True),
        lax.all_gather(w_up, "fsdp", axis=0, tiled=True),
        lax.all_gather(bias_up, "fsdp", axis=0, tiled=True),
        lax.all_gather(w_down, "fsdp", axis=0, tiled=True),
    )
    back_qkv, back_out, back_up, back_down = (again[2], again[3], again[4], again[6])
    grad_out = cotangent.astype(jnp.float32)
    grad_shift_down = jnp.sum(grad_out, axis=0)
    grad_down = contract_rows(hidden, cotangent)
    d_hidden = contract_cols(cotangent, back_down)
    d_up = gelu_pull(d_hidden)[0].astype(jnp.bfloat16)
    grad_up = contract_rows(normed_two, d_up)
    grad_bias_up = jnp.sum(d_up, axis=0, dtype=jnp.float32)
    d_normed_two = contract_cols(d_up, back_up)
    d_middle_norm, grad_gain_two, grad_shift_two = second_pull(d_normed_two)
    d_middle = grad_out + d_middle_norm
    grad_shift_out = jnp.sum(d_middle, axis=0)
    d_middle_low = d_middle.astype(jnp.bfloat16)
    grad_out_proj = contract_rows(mixed, d_middle_low)
    d_mixed = contract_cols(d_middle_low, back_out).astype(jnp.bfloat16)
    d_blocks = d_mixed.reshape(blocks_n, BLOCK, width)

    def backward_step(carry, entry):
        d_query, d_keys, d_values = attend_backward(
            entry[0], keys, values, entry[1], row_ids, entry[2], entry[3]
        )
        return ((carry[0] + d_keys, carry[1] + d_values), d_query)

    empty = jnp.zeros((rows_n, width), jnp.float32)
    (d_keys, d_values), d_query = lax.scan(
        backward_step, (empty, empty), (query_blocks, row_blocks, log_sums, d_blocks)
    )
    d_query = d_query.reshape(rows_n, width)
    d_qkv = jnp.concatenate([d_query, d_keys, d_values], axis=1).astype(jnp.bfloat16)
    grad_qkv = contract_rows(normed, d_qkv)
    grad_bias_query = jnp.sum(d_qkv[:, :width], axis=0, dtype=jnp.float32)
    grad_bias_value = jnp.sum(d_qkv[:, 2 * width :], axis=0, dtype=jnp.float32)
    d_normed = contract_cols(d_qkv, back_qkv)
    d_tokens_norm, grad_gain_one, grad_shift_one = norm_pull(d_normed)
    d_inputs = d_middle + d_tokens_norm
    grad_gains = jnp.stack([grad_gain_one, grad_gain_two])
    grad_shifts = jnp.stack(
        [
            grad_shift_one,
            grad_bias_query,
            grad_bias_value,
            grad_shift_out,
            grad_shift_two,
            grad_shift_down,
        ]
    )
    owned = (
        lax.psum_scatter(grad_gains, "fsdp", scatter_dimension=1, tiled=True),
        lax.psum_scatter(grad_shifts, "fsdp", scatter_dimension=1, tiled=True),
        lax.psum_scatter(grad_qkv, "fsdp", scatter_dimension=0, tiled=True),
        lax.psum_scatter(grad_out_proj, "fsdp", scatter_dimension=0, tiled=True),
        lax.psum_scatter(grad_up, "fsdp", scatter_dimension=0, tiled=True),
        lax.psum_scatter(grad_bias_up, "fsdp", scatter_dimension=0, tiled=True),
        lax.psum_scatter(grad_down, "fsdp", scatter_dimension=0, tiled=True),
    )
    summed = lax.psum((owned[0], owned[1], owned[2], owned[3], owned[4], owned[5], owned[6]), "dp")
    return (
        block_out,
        d_inputs,
        summed[0],
        summed[1],
        summed[2],
        summed[3],
        summed[4],
        summed[5],
        summed[6],
    )


def solution(mesh):
    placed = (
        P(("fsdp", "dp"), None),
        P(("fsdp", "dp")),
        P(None, "fsdp"),
        P(None, "fsdp"),
        P("fsdp", None),
        P("fsdp", None),
        P("fsdp", None),
        P("fsdp"),
        P("fsdp", None),
        P(("fsdp", "dp"), None),
    )
    return jax.shard_map(
        per_device,
        mesh=mesh,
        in_specs=placed,
        out_specs=(
            P(("fsdp", "dp"), None),
            P(("fsdp", "dp"), None),
            P(None, "fsdp"),
            P(None, "fsdp"),
            P("fsdp", None),
            P("fsdp", None),
            P("fsdp", None),
            P("fsdp"),
            P("fsdp", None),
        ),
        check_vma=False,
    )
```

profile of v0, /device:TPU:0, one launch (start us, length us, event | category | flops | bytes accessed | tf_op | source)
XLA Modules:
  0.0 1196.6 jit_solution(12556076253939985790)
XLA Ops:
  11.4 22.7 %all-gather = bf16[8,96,2]{1,2,0:T(2,128)(2,1)S(1)} all-gather(bf16[1,96,2]{1,2,0:T(2,128)(2,1)} %bitcast.158), channel_id=1, replica_groups=mesh['fsdp'=8,'dp'=4] {'fsdp'}, dimensions={0}, use_global_device_ids=true | all-gather | bytes 3456 | tf_op jit(solution)/shard_map/all_gather | solution.py:90
  34.9 26.7 %all-gather.2 = bf16[8,1,384]{2,1,0:T(2,128)(2,1)S(1)} all-gather(bf16[1,1,384]{2,1,0:T(2,128)(2,1)S(1)} %reshape.237), channel_id=1, replica_groups=mesh['fsdp'=8,'dp'=4] {'fsdp'}, dimensions={0}, use_global_device_ids=true | all-gather | bytes 6912 | tf_op jit(solution)/shard_map/all_gather | solution.py:95
  62.2 26.7 %all-gather.1 = bf16[8,96,6]{1,2,0:T(8,128)(2,1)S(1)} all-gather(bf16[1,96,6]{1,2,0:T(8,128)(2,1)} %bitcast.157), channel_id=1, replica_groups=mesh['fsdp'=8,'dp'=4] {'fsdp'}, dimensions={0}, use_global_device_ids=true | all-gather | bytes 10368 | tf_op jit(solution)/shard_map/all_gather | solution.py:91
  93.9 6.4 add_convert_fusion
  108.2 89.3 %while.27 = (s32[]{:T(128)}, bf16[2,512,768]{2,1,0:T(8,128)(2,1)}, f32[2,12,512]{2,1,0:T(8,128)S(1)}, s32[2,512]{1,0:T(2,128)S(1)}, s32[1024]{0:T(1024)S(1)}, /*...) while((s32[]{:T(128)}, bf16[2,512,768]{2,1,0:T(8,128)(2,1)}, ...), condition=%wide.region_5.6_spmd, body=%wide.region_2.5_spmd.sunk | while | flops 1686628352 | bytes 187926672 | solution.py:126
  109.7 10.6 fusion.103
  120.3 12.8 %fusion.104 = f32[12,512]{1,0:T(8,128)S(1)} fusion(f32[12,512,1024]{2,1,0:T(8,128)} %get-tuple-element.454, f32[12,512]{1,0:T(8,128)S(1)} %get-tuple-element.455, pred[512,1024]{1,0:T(8,128)(4,1)S(1)} %broadcast_compare_fusion.4), kind=kLoop, calls=%fused_computation.4.clone.1 | loop fusion | flops 25159680 | bytes 25739264 | tf_op jit(solution)/shard_map/while/body/eval_jaxpr/reduce_sum | solution.py:53
  136.3 9.0 fusion.105
  148.1 10.9 fusion.103
  159.1 12.4 %fusion.104 = f32[12,512]{1,0:T(8,128)S(1)} fusion(f32[12,512,1024]{2,1,0:T(8,128)} %get-tuple-element.454, f32[12,512]{1,0:T(8,128)S(1)} %get-tuple-element.455, pred[512,1024]{1,0:T(8,128)(4,1)S(1)} %broadcast_compare_fusion.4), kind=kLoop, calls=%fused_computation.4.clone.1 | loop fusion | flops 25159680 | bytes 25739264 | tf_op jit(solution)/shard_map/while/body/eval_jaxpr/reduce_sum | solution.py:53
  174.6 9.0 fusion.105
  197.5 3.9 fusion.49
  203.5 11.2 fusion.43
  214.7 65.3 %all-gather.14.cloned.1.call-done = bf16[3072,768]{1,0:T(8,128)(2,1)} async-done(((bf16[384,768]{1,0:T(8,128)(2,1)}), bf16[3072,768]{1,0:T(8,128)(2,1)}) %all-gather.14.cloned.1.call-update) | async-done | bytes 4718608 | tf_op jit(solution)/shard_map/all_gather | solution.py:96
  280.0 17.9 %convert_reduce_fusion = (f32[3072]{0:T(1024)}, bf16[1024,3072]{1,0:T(8,128)(2,1)S(1)}) fusion(f32[1024,3072]{1,0:T(8,128)} %fusion.43, f32[3072]{0:T(1024)S(1)} %bitcast.154, bf16[1024,768]{1,0:T(8,128)(2,1)S(1)} %copy-done.24, bf16[3072,768]{1,0:T(8,128)(2,1)} %all-gather.14.cloned.1.call-done), kind=kOutput, calls=%fused_computation.41 | convolution fusion | flops 4916769792 | bytes 25190400 | tf_op jit(solution)/shard_map/dot_general | solution.py:31
  297.9 7.3 fusion.51
  305.3 3.5 copy.88
  308.8 4.5 multiply_reduce_fusion.1
  319.7 3.9 convolution_convert_fusion
  324.8 179.8 %while.28 = (s32[]{:T(128)}, f32[1024,768]{0,1:T(8,128)}, f32[1024,768]{0,1:T(8,128)}, bf16[2,512,768]{2,1,0:T(8,128)(2,1)}, bf16[2,512,768]{1,2,0:T(8,128)(2,1)...) while((s32[]{:T(128)}, f32[1024,768]{0,1:T(8,128)}, ...), condition=%wide.region_12.13_spmd.clone, body=%wide.region_10.12_spmd.clone.sunk | while | flops 4126140416 | bytes 298764608 | solution.py:172
  329.2 10.3 fusion.116
  339.4 13.3 %fusion.117 = f32[12,64,1024]{2,1,0:T(8,128)} fusion(bf16[512,12,64]{0,2,1:T(8,128)(2,1)S(1)} %bitcast.137, f32[12,512,1024]{2,1,0:T(8,128)} %fusion.116, f32[12,512]{1,0:T(8,128)S(1)} %dynamic-slice_bitcast_fusion.2, pred[512,1024]{1,0:T(8,128)(4,1)S(1)} %broadcast_compare_fusion.5), kind=kOutput, calls=%fused_computation.17.clone.1 | convolution fusion | flops 830472192 | bytes 29646848 | tf_op jit(solution)/shard_map/while/body/eval_jaxpr/hqk,qhd->khd/dot_general | solution.py:66
  352.7 18.1 %multiply_reduce_fusion.5 = (f32[12,512]{1,0:T(8,128)S(1)}, f32[12,512,1024]{2,1,0:T(8,128)}) fusion(f32[12,512,1024]{2,1,0:T(8,128)} %fusion.116, f32[12,512]{1,0:T(8,128)S(1)} %dynamic-slice_bitcast_fusion.2, pred[512,1024]{1,0:T(8,128)(4,1)S(1)} %broadcast_compare_fusion.5, bf16[512,12,64]{0,2,1:T(8,128)(2,1)} %bitcast.136, ...), kind=kOutput, calls=%fused_computation.14.clone.1 | convolution fusion | flops 836757504 | bytes 53264384 | tf_op jit(solution)/shard_map/while/body/eval_jaxpr/qhd,khd->hqk/dot_general | solution.py:67
  370.8 21.8 %multiply_convert_fusion.2 = bf16[12,512,1024]{2,1,0:T(8,128)(2,1)} fusion(f32[12,512,1024]{2,1,0:T(8,128)} %get-tuple-element.467, f32[12,512,1024]{2,1,0:T(8,128)} %fusion.116, f32[12,512]{1,0:T(8,128)S(1)} %get-tuple-element.468, f32[12,512]{1,0:T(8,128)S(1)} %dynamic-slice_bitcast_fusion.2, pred[512,1024]{1,0:T(8,128)(4,1)S(1)} %broadcast_compare_fusion.5), kind=kLoop, calls=%fused_computation.13.clone.1 | loop fusion | flops 37748736 | bytes 63488000 | tf_op jit(solution)/shard_map/while/body/eval_jaxpr/convert_element_type | solution.py:71
  392.6 8.5 convolution_multiply_fusion.5
  401.1 7.0 convolution_multiply_fusion.4
  419.3 10.1 fusion.116
  429.4 13.0 %fusion.117 = f32[12,64,1024]{2,1,0:T(8,128)} fusion(bf16[512,12,64]{0,2,1:T(8,128)(2,1)S(1)} %bitcast.137, f32[12,512,1024]{2,1,0:T(8,128)} %fusion.116, f32[12,512]{1,0:T(8,128)S(1)} %dynamic-slice_bitcast_fusion.2, pred[512,1024]{1,0:T(8,128)(4,1)S(1)} %broadcast_compare_fusion.5), kind=kOutput, calls=%fused_computation.17.clone.1 | convolution fusion | flops 830472192 | bytes 29646848 | tf_op jit(solution)/shard_map/while/body/eval_jaxpr/hqk,qhd->khd/dot_general | solution.py:66
  442.4 18.1 %multiply_reduce_fusion.5 = (f32[12,512]{1,0:T(8,128)S(1)}, f32[12,512,1024]{2,1,0:T(8,128)}) fusion(f32[12,512,1024]{2,1,0:T(8,128)} %fusion.116, f32[12,512]{1,0:T(8,128)S(1)} %dynamic-slice_bitcast_fusion.2, pred[512,1024]{1,0:T(8,128)(4,1)S(1)} %broadcast_compare_fusion.5, bf16[512,12,64]{0,2,1:T(8,128)(2,1)} %bitcast.136, ...), kind=kOutput, calls=%fused_computation.14.clone.1 | convolution fusion | flops 836757504 | bytes 53264384 | tf_op jit(solution)/shard_map/while/body/eval_jaxpr/qhd,khd->hqk/dot_general | solution.py:67
  460.5 21.2 %multiply_convert_fusion.2 = bf16[12,512,1024]{2,1,0:T(8,128)(2,1)} fusion(f32[12,512,1024]{2,1,0:T(8,128)} %get-tuple-element.467, f32[12,512,1024]{2,1,0:T(8,128)} %fusion.116, f32[12,512]{1,0:T(8,128)S(1)} %get-tuple-element.468, f32[12,512]{1,0:T(8,128)S(1)} %dynamic-slice_bitcast_fusion.2, pred[512,1024]{1,0:T(8,128)(4,1)S(1)} %broadcast_compare_fusion.5), kind=kLoop, calls=%fused_computation.13.clone.1 | loop fusion | flops 37748736 | bytes 63488000 | tf_op jit(solution)/shard_map/while/body/eval_jaxpr/convert_element_type | solution.py:71
  481.7 8.5 convolution_multiply_fusion.5
  490.2 7.0 convolution_multiply_fusion.4
  504.6 3.2 copy.94
  509.6 9.8 fusion.31
  520.8 12.9 %fusion.44 = f32[3072,768]{1,0:T(8,128)} fusion(bf16[1024,768]{1,0:T(8,128)(2,1)S(1)} %copy-done.25, f32[1024,3072]{1,0:T(8,128)} %fusion.43, f32[3072]{0:T(1024)S(1)} %bitcast.155), kind=kOutput, calls=%fused_computation.105 | convolution fusion | flops 4863295488 | bytes 23605248 | tf_op jit(solution)/shard_map/dot_general | solution.py:25
  535.5 10.5 fusion.42
  548.0 8.0 fusion.50
  556.0 4.0 copy.96
  566.9 6.4 convert_reduce_fusion.2
  577.7 69.8 %reduce-scatter.11.cloned.1.call-done = f32[96,2304]{1,0:T(8,128)} async-done(((f32[768,2304]{1,0:T(8,128)}), f32[96,2304]{1,0:T(8,128)}) %reduce-scatter.11.cloned.1.call-update) | async-done | bytes 884752 | tf_op jit(solution)/shard_map/reduce_scatter | solution.py:197
  647.5 164.9 %reduce-scatter.17.cloned.1.call-done = f32[384,768]{1,0:T(8,128)} async-done(((f32[3072,768]{1,0:T(8,128)}), f32[384,768]{1,0:T(8,128)}) %reduce-scatter.17.cloned.1.call-update) | async-done | bytes 1179664 | tf_op jit(solution)/shard_map/reduce_scatter | solution.py:201
  812.3 164.8 %reduce-scatter.15.cloned.1.call-done = f32[96,3072]{1,0:T(8,128)} async-done(((f32[768,3072]{1,0:T(8,128)}), f32[96,3072]{1,0:T(8,128)}) %reduce-scatter.15.cloned.1.call-update) | async-done | bytes 1179664 | tf_op jit(solution)/shard_map/reduce_scatter | solution.py:199
  977.2 11.5 add_convert_fusion.1
  993.8 35.2 %all-reduce = f32[3072]{0:T(1024)S(1)} all-reduce(f32[3072]{0:T(1024)S(1)} %copy-done.51), channel_id=7, replica_groups=mesh['fsdp'=8,'dp'=4] {'fsdp'}, use_global_device_ids=true, to_apply=%region_34.35.clone | all-reduce | flops 3072 | bytes 24576
  1029.1 13.3 %reduce-scatter.19.cloned.1.call-done = f32[96,2]{1,0:T(8,128)} async-done(((f32[768,2]{1,0:T(8,128)}), f32[96,2]{1,0:T(8,128)}) %reduce-scatter.19.cloned.1.call-update) | async-done | bytes 784
  1043.2 64.1 %reduce-scatter.21.cloned.1.call-done = f32[96,6]{1,0:T(8,128)} async-done(((f32[768,6]{1,0:T(8,128)}), f32[96,6]{1,0:T(8,128)}) %reduce-scatter.21.cloned.1.call-update) | async-done | bytes 2320
  1108.2 6.3 all-reduce.1
  1114.5 69.3 %all-reduce.5.cloned.1.call-done = (f32[96,2304]{1,0:T(8,128)}, f32[96,768]{1,0:T(8,128)}, f32[96,3072]{1,0:T(8,128)}, f32[384,768]{1,0:T(8,128)}) async-done(((f32[96,2304]{1,0:T(8,128)}, f32[96,768]{1,0:T(8,128)}, f32[96,3072]{1,0:T(8,128)}, f32[384,768]{1,0:T(8,128)}), (f32[96,2304]{1,0:T(8,128)}, f32[96,768]{1,0:T(8,128)}, f32[96,3072]{1,0:T(8,128)}, f32[384,768]{1,0:T(8,128)})) %all-reduce.5.cloned.1.call-update) | async-done | bytes 3538960 | tf_op jit(solution)/shard_map/psum | solution.py:203
  (251 shorter events, 92.2 us)
Async XLA Ops:
  7.2 86.7 %all-gather.8.cloned.1.call-start = ((), (), s32[]{:S(2)}) async-start(), calls=%async_computation.6 | async-start | bytes 3981312 | tf_op jit(solution)/shard_map/all_gather | solution.py:92
  7.9 189.5 %all-gather.10.cloned.1.call-start = ((), (), s32[]{:S(2)}) async-start(), calls=%async_computation.7 | async-start | bytes 1327104 | tf_op jit(solution)/shard_map/all_gather | solution.py:93
  8.7 194.8 %all-gather.12.cloned.1.call-start = ((), (), s32[]{:S(2)}) async-start(), calls=%async_computation.8 | async-start | bytes 5308416 | tf_op jit(solution)/shard_map/all_gather | solution.py:94
  9.4 270.6 %all-gather.14.cloned.1.call-start = ((), (), s32[]{:S(2)}) async-start(), calls=%async_computation.9 | async-start | bytes 5308416 | tf_op jit(solution)/shard_map/all_gather | solution.py:96
  10.0 567.7 %reduce-scatter.13.cloned.1.call-start = ((), (), s32[]{:S(2)}) async-start(), calls=%async_computation.11 | async-start | bytes 2654208 | tf_op jit(solution)/shard_map/reduce_scatter | solution.py:198
  34.9 59.1 %copy-start.40 = (f32[768]{0:T(1024)}, f32[768]{0:T(1024)S(1)}, u32[]{:S(2)}) copy-start(f32[768]{0:T(1024)S(1)} %get-tuple-element.277) | copy-start | bytes 9220
  89.6 4.3 copy-start.54
  91.8 8.6 copy-start.38
  92.2 8.2 copy-start.44
  92.2 8.1 copy-start.42
  105.3 2.9 copy-start.31
  108.1 89.3 %copy-start.56 = (f32[768]{0:T(1024)S(1)}, f32[768]{0:T(1024)}, u32[]{:S(2)}) copy-start(f32[768]{0:T(1024)} %get-tuple-element.272) | copy-start | bytes 9220
  120.3 16.0 %copy-start = (f32[12,512,1024]{2,1,0:T(8,128)S(1)}, f32[12,512,1024]{2,1,0:T(8,128)}, u32[]{:S(2)}) copy-start(f32[12,512,1024]{2,1,0:T(8,128)} %get-tuple-element.454) | copy-start | bytes 75497472 | tf_op jit(solution)/shard_map/while
  159.1 15.5 %copy-start = (f32[12,512,1024]{2,1,0:T(8,128)S(1)}, f32[12,512,1024]{2,1,0:T(8,128)}, u32[]{:S(2)}) copy-start(f32[12,512,1024]{2,1,0:T(8,128)} %get-tuple-element.454) | copy-start | bytes 75497472 | tf_op jit(solution)/shard_map/while
  201.4 111.9 %copy-start.29 = (f32[1024]{0:T(1024)}, f32[1024]{0:T(1024)S(1)}, u32[]{:S(2)}) copy-start(f32[1024]{0:T(1024)S(1)} %broadcast_multiply_fusion) | copy-start | bytes 12292
  203.5 109.8 %copy-start.34 = (f32[1024]{0:T(1024)}, f32[1024]{0:T(1024)S(1)}, u32[]{:S(2)}) copy-start(f32[1024]{0:T(1024)S(1)} %fusion.37) | copy-start | bytes 12292
  203.5 76.5 %copy-start.24 = (bf16[1024,768]{1,0:T(8,128)(2,1)S(1)}, bf16[1024,768]{1,0:T(8,128)(2,1)}, u32[]{:S(2)}) copy-start(bf16[1024,768]{1,0:T(8,128)(2,1)} %param.23) | copy-start | bytes 4718596
  203.5 76.5 %copy-start.49 = (f32[8,1,384]{2,1,0:T(1,128)S(1)}, f32[8,1,384]{2,1,0:T(1,128)}, u32[]{:S(2)}) copy-start(f32[8,1,384]{2,1,0:T(1,128)} %convert_element_type.84) | copy-start | bytes 36868
  280.0 17.9 %copy-start.22 = (bf16[768,3072]{1,0:T(8,128)(2,1)S(1)}, bf16[768,3072]{1,0:T(8,128)(2,1)}, u32[]{:S(2)}) copy-start(bf16[768,3072]{1,0:T(8,128)(2,1)} %all-gather.12.cloned.1.call-done) | copy-start | bytes 14155780
  297.9 7.3 copy-start.58
  308.8 4.5 copy-start.11
  308.8 4.7 copy-start.16
  319.6 327.8 %reduce-scatter.11.cloned.1.call-start = ((), (), s32[]{:S(2)}) async-start(), calls=%async_computation.10 | async-start | bytes 7962624 | tf_op jit(solution)/shard_map/reduce_scatter | solution.py:197
  329.1 10.3 copy-start.7
  401.1 7.1 copy-start.1
  401.1 7.1 copy-start.4
  401.1 7.3 copy-start.6
  419.3 10.1 copy-start.7
  490.2 7.1 copy-start.1
  490.2 7.1 copy-start.4
  490.2 7.3 copy-start.6
  504.6 3.3 copy-start.3
  519.4 293.0 %reduce-scatter.17.cloned.1.call-start = ((), (), s32[]{:S(2)}) async-start(), calls=%async_computation.13 | async-start | bytes 10616832 | tf_op jit(solution)/shard_map/reduce_scatter | solution.py:201
  533.7 443.5 %reduce-scatter.15.cloned.1.call-start = ((), (), s32[]{:S(2)}) async-start(), calls=%async_computation.12 | async-start | bytes 10616832 | tf_op jit(solution)/shard_map/reduce_scatter | solution.py:199
  546.1 496.3 %reduce-scatter.19.cloned.1.call-start = ((), (), s32[]{:S(2)}) async-start(), calls=%async_computation.14 | async-start | bytes 442368
  556.0 4.0 copy-start.9
  560.0 2.9 copy-start.14
  562.9 4.0 copy-start.18
  562.9 4.0 copy-start.47
  566.9 8.4 copy-start.52
  566.9 9.5 copy-start.57
  573.3 403.9 %copy-start.13 = (f32[1024,768]{0,1:T(8,128)S(1)}, f32[1024,768]{0,1:T(8,128)}, u32[]{:S(2)}) copy-start(f32[1024,768]{0,1:T(8,128)} %copy-done.10) | copy-start | bytes 9437188
  573.3 403.9 %copy-start.53 = (f32[768]{0:T(1024)S(1)}, f32[768]{0:T(1024)}, u32[]{:S(2)}) copy-start(f32[768]{0:T(1024)} %get-tuple-element.271) | copy-start | bytes 9220
  573.4 533.9 %reduce-scatter.21.cloned.1.call-start = ((), (), s32[]{:S(2)}) async-start(), calls=%async_computation.15 | async-start | bytes 442368
  576.3 607.5 %all-reduce.5.cloned.1.call-start = ((), (), s32[]{:S(2)}) async-start(), calls=%async_computation.16 | async-start | bytes 7077888 | tf_op jit(solution)/shard_map/psum | solution.py:203
  988.7 2.7 copy-start.19
  1183.8 4.0 copy-start.28
  1183.8 5.0 copy-start.27
  (29 other events, 52.5 us)
Sparse Core Ops, SparseCore 0:
  10.2 67.5 all-gather.7
  79.9 40.0 all-gather.9
  122.2 78.0 all-gather.11
  202.3 77.6 all-gather.13
  319.8 67.9 reduce-scatter.12
  519.5 127.9 reduce-scatter.10
  651.1 161.2 reduce-scatter.16
  815.9 161.1 reduce-scatter.14
  981.0 61.2 reduce-scatter.18
  1046.0 61.2 reduce-scatter.20
  1109.9 73.8 all-reduce.4
where the time goes:
time: 1210 us; the launch traced here: 1200 us
  waiting for transfers between devices  614 us (51%)
  matrix products  259 us (21%)
  blocking collectives  118 us (10%)
  other arithmetic  95.8 us (8%)
  local copies, waits for them, and re-layouts  80.1 us (7%)
  between operations  15.3 us (1%)
  loops' own time  13.4 us (1%)
    reduce_scatter x1, waiting for transfers between devices, per_device(): lax.psum_scatter(grad_down, 'fsdp', scatter_dimension=0, tiled=True)  165 us
    reduce_scatter x1, waiting for transfers between devices, per_device(): lax.psum_scatter(grad_up, 'fsdp', scatter_dimension=0, tiled=True)  165 us
    unnamed x13, waiting for transfers between devices  80 us
    reduce_scatter x1, waiting for transfers between devices, per_device(): lax.psum_scatter(grad_qkv, 'fsdp', scatter_dimension=0, tiled=True)  69.8 us
    psum x1, waiting for transfers between devices, per_device(): lax.psum((owned[0], owned[1], owned[2], owned[3], owned[4], owned[5], own...  69.3 us
    all_gather x1, waiting for transfers between devices, per_device(): lax.all_gather(w_down, 'fsdp', axis=0, tiled=True)  65.3 us
    convert_element_type x2, other arithmetic, attend_backward(): d_scores = (attn_probs * (d_probs - inner)).astype(jnp.bfloat16)  43 us
    dot_general x4, matrix products, block_scores(): jnp.einsum('qhd,khd->hqk', split_heads(query), split_heads(keys), preferr...  41.9 us
  transfers between devices with their start and end apart: 11, of which 7 were waited for; matrix products, arithmetic and copies ran while one was open for 31% of the time, Pallas kernels for 0%

commit v1 on v0

--- a/solution.py
+++ b/solution.py
@@ -8,6 +8,18 @@
 HEAD = 64
 BLOCK = 512
 norm_eps = 1e-05
+
+
+def collect(x, axis, dim):
+    ways, here, hop = (lax.axis_size(axis), lax.axis_index(axis), x.shape[dim])
+    line, have = (x, 1)
+    while have < ways:
+        line = jnp.concatenate(
+            [line, lax.ppermute(line, axis, [(d, (d - have) % ways) for d in range(ways)])],
+            axis=dim,
+        )
+        have = 2 * have
+    return jnp.roll(line, here * hop, axis=dim)
 
 
 def layer_norm(values, gain, shift):
@@ -92,7 +104,7 @@
         lax.all_gather(w_qkv, "fsdp", axis=0, tiled=True),
         lax.all_gather(w_out, "fsdp", axis=0, tiled=True),
         lax.all_gather(w_up, "fsdp", axis=0, tiled=True),
-        lax.all_gather(bias_up, "fsdp", axis=0, tiled=True),
+        collect(bias_up, "fsdp", 0),
         lax.all_gather(w_down, "fsdp", axis=0, tiled=True),
     )
     gains = gathered[0].astype(jnp.float32)

time: 1210 us -> 1200 us (level)
  waiting for transfers between devices: 614 us -> 652 us
  blocking collectives: 118 us -> 85.8 us
  loops' own time: 13.4 us -> 1.29 us
    all_gather x1 -> x0, blocking collectives: 26.7 us -> none  [per_device(): lax.all_gather(bias_up, 'fsdp', axis=0, tiled=True)]
    all_gather x1, waiting for transfers between devices: 0.02 us -> 25.2 us  [per_device(): lax.all_gather(w_up, 'fsdp', axis=0, tiled=True)]
    another operation x1, loops' own time: 12.7 us -> 0.54 us  [per_device(): mixed, log_sums = lax.map(forward_block, (query_blocks, row_blocks))]
    unnamed x119 -> x127, local copies, waits for them, and re-layouts: 28.5 us -> 29.3 us
  transfers between devices with their start and end apart: 11 -> 14, of which waited for: 7 -> 11; matrix products, arithmetic and copies ran while one was open for 31% -> 31% of each run, Pallas kernels for 0% -> 0%
where the time goes in v1:
time: 1200 us
  waiting for transfers between devices  652 us (54%)
  matrix products  259 us (22%)
  other arithmetic  95.5 us (8%)
  blocking collectives  85.8 us (7%)
  local copies, waits for them, and re-layouts  80.9 us (7%)
  between operations  15.4 us (1%)
    reduce_scatter x1, waiting for transfers between devices, per_device(): lax.psum_scatter(grad_down, 'fsdp', scatter_dimension=0, tiled=True)  165 us
    reduce_scatter x1, waiting for transfers between devices, per_device(): lax.psum_scatter(grad_up, 'fsdp', scatter_dimension=0, tiled=True)  165 us
    unnamed x13, waiting for transfers between devices  79.5 us
    reduce_scatter x1, waiting for transfers between devices, per_device(): lax.psum_scatter(grad_qkv, 'fsdp', scatter_dimension=0, tiled=True)  69.8 us
    psum x1, waiting for transfers between devices, per_device(): lax.psum((owned[0], owned[1], owned[2], owned[3], owned[4], owned[5], own...  69.4 us
    all_gather x1, waiting for transfers between devices, per_device(): lax.all_gather(w_down, 'fsdp', axis=0, tiled=True)  68.6 us
    convert_element_type x2, other arithmetic, attend_backward(): d_scores = (attn_probs * (d_probs - inner)).astype(jnp.bfloat16)  43 us
    dot_general x4, matrix products, block_scores(): jnp.einsum('qhd,khd->hqk', split_heads(query), split_heads(keys), preferr...  41.7 us
  transfers between devices with their start and end apart: 14, of which 11 were waited for; matrix products, arithmetic and copies ran while one was open for 31% of the time, Pallas kernels for 0%

profile of v1, /device:TPU:0, one launch (start us, length us, event | category | flops | bytes accessed | tf_op | source)
XLA Modules:
  0.0 1196.8 jit_solution(8009775883081099555)
XLA Ops:
  9.4 6.1 collective-permute-start
  15.6 17.3 %all-gather = bf16[8,96,2]{1,2,0:T(2,128)(2,1)S(1)} all-gather(bf16[1,96,2]{1,2,0:T(2,128)(2,1)} %bitcast.154), channel_id=1, replica_groups=mesh['fsdp'=8,'dp'=4] {'fsdp'}, dimensions={0}, use_global_device_ids=true | all-gather | bytes 3456 | tf_op jit(solution)/shard_map/all_gather | solution.py:102
  32.8 27.1 %all-gather.1 = bf16[8,96,6]{1,2,0:T(8,128)(2,1)S(1)} all-gather(bf16[1,96,6]{1,2,0:T(8,128)(2,1)} %bitcast.153), channel_id=1, replica_groups=mesh['fsdp'=8,'dp'=4] {'fsdp'}, dimensions={0}, use_global_device_ids=true | all-gather | bytes 10368 | tf_op jit(solution)/shard_map/all_gather | solution.py:103
  73.8 4.0 all-gather.7.cloned.1.call-done
  77.8 6.4 add_convert_fusion
  91.9 77.0 %while.27 = (s32[]{:T(128)}, bf16[2,512,768]{2,1,0:T(8,128)(2,1)}, f32[2,12,512]{2,1,0:T(8,128)S(1)}, s32[2,512]{1,0:T(2,128)S(1)}, s32[1024]{0:T(1024)S(1)}, /*...) while((s32[]{:T(128)}, bf16[2,512,768]{2,1,0:T(8,128)(2,1)}, ...), condition=%wide.region_5.6_spmd, body=%wide.region_2.5_spmd.sunk | while | flops 1686628352 | bytes 187926672 | solution.py:138
  94.0 10.7 fusion.103
  104.7 12.4 %fusion.104 = f32[12,512]{1,0:T(8,128)S(1)} fusion(f32[12,512,1024]{2,1,0:T(8,128)} %get-tuple-element.454, f32[12,512]{1,0:T(8,128)S(1)} %get-tuple-element.455, pred[512,1024]{1,0:T(8,128)(4,1)S(1)} %broadcast_compare_fusion.4), kind=kLoop, calls=%fused_computation.4.clone.1 | loop fusion | flops 25159680 | bytes 25739264 | tf_op jit(solution)/shard_map/while/body/eval_jaxpr/reduce_sum | solution.py:65
  120.2 9.0 fusion.105
  132.0 10.7 fusion.103
  142.7 12.3 %fusion.104 = f32[12,512]{1,0:T(8,128)S(1)} fusion(f32[12,512,1024]{2,1,0:T(8,128)} %get-tuple-element.454, f32[12,512]{1,0:T(8,128)S(1)} %get-tuple-element.455, pred[512,1024]{1,0:T(8,128)(4,1)S(1)} %broadcast_compare_fusion.4), kind=kLoop, calls=%fused_computation.4.clone.1 | loop fusion | flops 25159680 | bytes 25739264 | tf_op jit(solution)/shard_map/while/body/eval_jaxpr/reduce_sum | solution.py:65
  158.7 9.0 fusion.105
  169.0 3.9 fusion.49
  174.9 25.2 %all-gather.11.cloned.1.call-done = bf16[768,3072]{1,0:T(8,128)(2,1)} async-done(((bf16[96,3072]{1,0:T(8,128)(2,1)}), bf16[768,3072]{1,0:T(8,128)(2,1)}) %all-gather.11.cloned.1.call-update) | async-done | bytes 4718608 | tf_op jit(solution)/shard_map/all_gather | solution.py:106
  200.1 11.2 fusion.43
  211.3 68.6 %all-gather.13.cloned.1.call-done = bf16[3072,768]{1,0:T(8,128)(2,1)} async-done(((bf16[384,768]{1,0:T(8,128)(2,1)}), bf16[3072,768]{1,0:T(8,128)(2,1)}) %all-gather.13.cloned.1.call-update) | async-done | bytes 4718608 | tf_op jit(solution)/shard_map/all_gather | solution.py:108
  279.9 18.1 %convert_reduce_fusion = (f32[3072]{0:T(1024)}, bf16[1024,3072]{1,0:T(8,128)(2,1)S(1)}) fusion(f32[1024,3072]{1,0:T(8,128)} %fusion.43, f32[3072]{0:T(1024)S(1)} %copy-done.50, bf16[1024,768]{1,0:T(8,128)(2,1)S(1)} %copy-done.24, bf16[3072,768]{1,0:T(8,128)(2,1)} %all-gather.13.cloned.1.call-done), kind=kOutput, calls=%fused_computation.41 | convolution fusion | flops 4916769792 | bytes 25190400 | tf_op jit(solution)/shard_map/dot_general | solution.py:43
  298.0 7.3 fusion.51
  308.9 4.5 multiply_reduce_fusion.1
  319.8 3.9 convolution_convert_fusion
  324.9 179.8 %while.28 = (s32[]{:T(128)}, f32[1024,768]{0,1:T(8,128)}, f32[1024,768]{0,1:T(8,128)}, bf16[2,512,768]{2,1,0:T(8,128)(2,1)}, bf16[2,512,768]{1,2,0:T(8,128)(2,1)...) while((s32[]{:T(128)}, f32[1024,768]{0,1:T(8,128)}, ...), condition=%wide.region_12.13_spmd.clone, body=%wide.region_10.12_spmd.clone.sunk | while | flops 4126140416 | bytes 298764608 | solution.py:184
  329.3 10.2 fusion.116
  339.5 13.3 %fusion.117 = f32[12,64,1024]{2,1,0:T(8,128)} fusion(bf16[512,12,64]{0,2,1:T(8,128)(2,1)S(1)} %bitcast.136, f32[12,512,1024]{2,1,0:T(8,128)} %fusion.116, f32[12,512]{1,0:T(8,128)S(1)} %dynamic-slice_bitcast_fusion.2, pred[512,1024]{1,0:T(8,128)(4,1)S(1)} %broadcast_compare_fusion.5), kind=kOutput, calls=%fused_computation.17.clone.1 | convolution fusion | flops 830472192 | bytes 29646848 | tf_op jit(solution)/shard_map/while/body/eval_jaxpr/hqk,qhd->khd/dot_general | solution.py:78
  352.8 18.1 %multiply_reduce_fusion.5 = (f32[12,512]{1,0:T(8,128)S(1)}, f32[12,512,1024]{2,1,0:T(8,128)}) fusion(f32[12,512,1024]{2,1,0:T(8,128)} %fusion.116, f32[12,512]{1,0:T(8,128)S(1)} %dynamic-slice_bitcast_fusion.2, pred[512,1024]{1,0:T(8,128)(4,1)S(1)} %broadcast_compare_fusion.5, bf16[512,12,64]{0,2,1:T(8,128)(2,1)} %bitcast.135, ...), kind=kOutput, calls=%fused_computation.14.clone.1 | convolution fusion | flops 836757504 | bytes 53264384 | tf_op jit(solution)/shard_map/while/body/eval_jaxpr/qhd,khd->hqk/dot_general | solution.py:79
  370.9 21.8 %multiply_convert_fusion.2 = bf16[12,512,1024]{2,1,0:T(8,128)(2,1)} fusion(f32[12,512,1024]{2,1,0:T(8,128)} %get-tuple-element.467, f32[12,512,1024]{2,1,0:T(8,128)} %fusion.116, f32[12,512]{1,0:T(8,128)S(1)} %get-tuple-element.468, f32[12,512]{1,0:T(8,128)S(1)} %dynamic-slice_bitcast_fusion.2, pred[512,1024]{1,0:T(8,128)(4,1)S(1)} %broadcast_compare_fusion.5), kind=kLoop, calls=%fused_computation.13.clone.1 | loop fusion | flops 37748736 | bytes 63488000 | tf_op jit(solution)/shard_map/while/body/eval_jaxpr/convert_element_type | solution.py:83
  392.7 8.5 convolution_multiply_fusion.5
  401.2 7.0 convolution_multiply_fusion.4
  419.4 10.1 fusion.116
  429.5 13.0 %fusion.117 = f32[12,64,1024]{2,1,0:T(8,128)} fusion(bf16[512,12,64]{0,2,1:T(8,128)(2,1)S(1)} %bitcast.136, f32[12,512,1024]{2,1,0:T(8,128)} %fusion.116, f32[12,512]{1,0:T(8,128)S(1)} %dynamic-slice_bitcast_fusion.2, pred[512,1024]{1,0:T(8,128)(4,1)S(1)} %broadcast_compare_fusion.5), kind=kOutput, calls=%fused_computation.17.clone.1 | convolution fusion | flops 830472192 | bytes 29646848 | tf_op jit(solution)/shard_map/while/body/eval_jaxpr/hqk,qhd->khd/dot_general | solution.py:78
  442.5 18.1 %multiply_reduce_fusion.5 = (f32[12,512]{1,0:T(8,128)S(1)}, f32[12,512,1024]{2,1,0:T(8,128)}) fusion(f32[12,512,1024]{2,1,0:T(8,128)} %fusion.116, f32[12,512]{1,0:T(8,128)S(1)} %dynamic-slice_bitcast_fusion.2, pred[512,1024]{1,0:T(8,128)(4,1)S(1)} %broadcast_compare_fusion.5, bf16[512,12,64]{0,2,1:T(8,128)(2,1)} %bitcast.135, ...), kind=kOutput, calls=%fused_computation.14.clone.1 | convolution fusion | flops 836757504 | bytes 53264384 | tf_op jit(solution)/shard_map/while/body/eval_jaxpr/qhd,khd->hqk/dot_general | solution.py:79
  460.5 21.2 %multiply_convert_fusion.2 = bf16[12,512,1024]{2,1,0:T(8,128)(2,1)} fusion(f32[12,512,1024]{2,1,0:T(8,128)} %get-tuple-element.467, f32[12,512,1024]{2,1,0:T(8,128)} %fusion.116, f32[12,512]{1,0:T(8,128)S(1)} %get-tuple-element.468, f32[12,512]{1,0:T(8,128)S(1)} %dynamic-slice_bitcast_fusion.2, pred[512,1024]{1,0:T(8,128)(4,1)S(1)} %broadcast_compare_fusion.5), kind=kLoop, calls=%fused_computation.13.clone.1 | loop fusion | flops 37748736 | bytes 63488000 | tf_op jit(solution)/shard_map/while/body/eval_jaxpr/convert_element_type | solution.py:83
  481.8 8.5 convolution_multiply_fusion.5
  490.3 7.0 convolution_multiply_fusion.4
  509.7 9.8 fusion.31
  520.9 12.9 %fusion.44 = f32[3072,768]{1,0:T(8,128)} fusion(bf16[1024,768]{1,0:T(8,128)(2,1)S(1)} %copy-done.25, f32[1024,3072]{1,0:T(8,128)} %fusion.43, f32[3072]{0:T(1024)S(1)} %copy-done.51), kind=kOutput, calls=%fused_computation.108 | convolution fusion | flops 4863295488 | bytes 23605248 | tf_op jit(solution)/shard_map/dot_general | solution.py:37
  535.7 10.5 fusion.42
  548.1 8.0 fusion.50
  556.1 4.0 copy.96
  567.1 6.4 convert_reduce_fusion.2
  577.8 69.8 %reduce-scatter.11.cloned.1.call-done = f32[96,2304]{1,0:T(8,128)} async-done(((f32[768,2304]{1,0:T(8,128)}), f32[96,2304]{1,0:T(8,128)}) %reduce-scatter.11.cloned.1.call-update) | async-done | bytes 884752 | tf_op jit(solution)/shard_map/reduce_scatter | solution.py:209
  647.6 164.9 %reduce-scatter.17.cloned.1.call-done = f32[384,768]{1,0:T(8,128)} async-done(((f32[3072,768]{1,0:T(8,128)}), f32[384,768]{1,0:T(8,128)}) %reduce-scatter.17.cloned.1.call-update) | async-done | bytes 1179664 | tf_op jit(solution)/shard_map/reduce_scatter | solution.py:213
  812.5 164.9 %reduce-scatter.15.cloned.1.call-done = f32[96,3072]{1,0:T(8,128)} async-done(((f32[768,3072]{1,0:T(8,128)}), f32[96,3072]{1,0:T(8,128)}) %reduce-scatter.15.cloned.1.call-update) | async-done | bytes 1179664 | tf_op jit(solution)/shard_map/reduce_scatter | solution.py:211
  977.4 11.5 add_convert_fusion.1
  994.0 35.2 %all-reduce = f32[3072]{0:T(1024)S(1)} all-reduce(f32[3072]{0:T(1024)S(1)} %copy-done.52), channel_id=7, replica_groups=mesh['fsdp'=8,'dp'=4] {'fsdp'}, use_global_device_ids=true, to_apply=%region_34.35.clone | all-reduce | flops 3072 | bytes 24576
  1029.3 13.2 %reduce-scatter.19.cloned.1.call-done = f32[96,2]{1,0:T(8,128)} async-done(((f32[768,2]{1,0:T(8,128)}), f32[96,2]{1,0:T(8,128)}) %reduce-scatter.19.cloned.1.call-update) | async-done | bytes 784
  1043.4 64.1 %reduce-scatter.21.cloned.1.call-done = f32[96,6]{1,0:T(8,128)} async-done(((f32[768,6]{1,0:T(8,128)}), f32[96,6]{1,0:T(8,128)}) %reduce-scatter.21.cloned.1.call-update) | async-done | bytes 2320
  1108.3 6.3 all-reduce.1
  1114.6 69.4 %all-reduce.5.cloned.1.call-done = (f32[96,2304]{1,0:T(8,128)}, f32[96,768]{1,0:T(8,128)}, f32[96,3072]{1,0:T(8,128)}, f32[384,768]{1,0:T(8,128)}) async-done(((f32[96,2304]{1,0:T(8,128)}, f32[96,768]{1,0:T(8,128)}, f32[96,3072]{1,0:T(8,128)}, f32[384,768]{1,0:T(8,128)}), (f32[96,2304]{1,0:T(8,128)}, f32[96,768]{1,0:T(8,128)}, f32[96,3072]{1,0:T(8,128)}, f32[384,768]{1,0:T(8,128)})) %all-reduce.5.cloned.1.call-update) | async-done | bytes 3538960 | tf_op jit(solution)/shard_map/psum | solution.py:215
  (268 shorter events, 104.9 us)
Async XLA Ops:
  7.2 70.7 %all-gather.7.cloned.1.call-start = ((), (), s32[]{:S(2)}) async-start(), calls=%async_computation.6 | async-start | bytes 3981312 | tf_op jit(solution)/shard_map/all_gather | solution.py:104
  7.9 161.1 %all-gather.9.cloned.1.call-start = ((), (), s32[]{:S(2)}) async-start(), calls=%async_computation.7 | async-start | bytes 1327104 | tf_op jit(solution)/shard_map/all_gather | solution.py:105
  8.7 191.5 %all-gather.11.cloned.1.call-start = ((), (), s32[]{:S(2)}) async-start(), calls=%async_computation.8 | async-start | bytes 5308416 | tf_op jit(solution)/shard_map/all_gather | solution.py:106
  9.4 270.5 %all-gather.13.cloned.1.call-start = ((), (), s32[]{:S(2)}) async-start(), calls=%async_computation.9 | async-start | bytes 5308416 | tf_op jit(solution)/shard_map/all_gather | solution.py:108
  9.4 53.9 %collective-permute-start = (bf16[384]{0:T(512)(128)(2,1)}, bf16[384]{0:T(512)(128)(2,1)S(1)}, u32[]{:S(2)}, u32[]{:S(2)}) collective-permute-start(bf16[384]{0:T(512)(128)(2,1)} %param.21), channel_id=1, source_target_pairs={{0,28},{4,0},{8,4},{12,8},{16,12},{20,16},{24,20},{28,24},{1,29},{... | collective-permute-start | bytes 2312 | tf_op jit(solution)/shard_map/ppermute | solution.py:18
  15.5 562.3 %reduce-scatter.13.cloned.1.call-start = ((), (), s32[]{:S(2)}) async-start(), calls=%async_computation.11 | async-start | bytes 2654208 | tf_op jit(solution)/shard_map/reduce_scatter | solution.py:210
  60.0 7.2 copy-start.31
  60.0 7.2 copy-start.23
  61.8 16.0 %copy-start.8 = (bf16[1024,768]{0,1:T(8,128)(2,1)}, bf16[1024,768]{0,1:T(8,128)(2,1)S(1)}, u32[]{:S(2)}) copy-start(bf16[1024,768]{0,1:T(8,128)(2,1)S(1)} %copy.79) | copy-start | bytes 4718596
  62.1 22.1 %copy-start.38 = (f32[1024]{0:T(1024)}, f32[1024]{0:T(1024)S(1)}, u32[]{:S(2)}) copy-start(f32[1024]{0:T(1024)S(1)} %broadcast_multiply_fusion.1) | copy-start | bytes 12292
  62.6 4.5 copy-start.44
  62.6 21.6 %copy-start.42 = (f32[1024]{0:T(1024)}, f32[1024]{0:T(1024)S(1)}, u32[]{:S(2)}) copy-start(f32[1024]{0:T(1024)S(1)} %fusion.36) | copy-start | bytes 12292
  63.2 21.0 %copy-start.55 = (f32[768]{0:T(1024)}, f32[768]{0:T(1024)S(1)}, u32[]{:S(2)}) copy-start(f32[768]{0:T(1024)S(1)} %get-tuple-element.275) | copy-start | bytes 9220
  63.4 3.6 collective-permute-start.1
  64.0 20.2 %copy-start.40 = (f32[768]{0:T(1024)}, f32[768]{0:T(1024)S(1)}, u32[]{:S(2)}) copy-start(f32[768]{0:T(1024)S(1)} %get-tuple-element.277) | copy-start | bytes 9220
  67.0 5.1 collective-permute-start.2
  91.9 77.0 %copy-start.57 = (f32[768]{0:T(1024)S(1)}, f32[768]{0:T(1024)}, u32[]{:S(2)}) copy-start(f32[768]{0:T(1024)} %get-tuple-element.272) | copy-start | bytes 9220
  104.7 15.5 %copy-start = (f32[12,512,1024]{2,1,0:T(8,128)S(1)}, f32[12,512,1024]{2,1,0:T(8,128)}, u32[]{:S(2)}) copy-start(f32[12,512,1024]{2,1,0:T(8,128)} %get-tuple-element.454) | copy-start | bytes 75497472 | tf_op jit(solution)/shard_map/while
  142.7 16.0 %copy-start = (f32[12,512,1024]{2,1,0:T(8,128)S(1)}, f32[12,512,1024]{2,1,0:T(8,128)}, u32[]{:S(2)}) copy-start(f32[12,512,1024]{2,1,0:T(8,128)} %get-tuple-element.454) | copy-start | bytes 75497472 | tf_op jit(solution)/shard_map/while
  172.9 27.2 %copy-start.32 = (f32[768]{0:T(1024)S(1)}, f32[768]{0:T(1024)}, u32[]{:S(2)}) copy-start(f32[768]{0:T(1024)} %get-tuple-element.276) | copy-start | bytes 9220
  172.9 27.2 %copy-start.36 = (f32[768]{0:T(1024)S(1)}, f32[768]{0:T(1024)}, u32[]{:S(2)}) copy-start(f32[768]{0:T(1024)} %get-tuple-element.270) | copy-start | bytes 9220
  172.9 140.5 %copy-start.29 = (f32[1024]{0:T(1024)}, f32[1024]{0:T(1024)S(1)}, u32[]{:S(2)}) copy-start(f32[1024]{0:T(1024)S(1)} %broadcast_multiply_fusion) | copy-start | bytes 12292
  174.9 138.5 %copy-start.34 = (f32[1024]{0:T(1024)}, f32[1024]{0:T(1024)S(1)}, u32[]{:S(2)}) copy-start(f32[1024]{0:T(1024)S(1)} %fusion.37) | copy-start | bytes 12292
  200.1 79.8 %copy-start.24 = (bf16[1024,768]{1,0:T(8,128)(2,1)S(1)}, bf16[1024,768]{1,0:T(8,128)(2,1)}, u32[]{:S(2)}) copy-start(bf16[1024,768]{1,0:T(8,128)(2,1)} %param.23) | copy-start | bytes 4718596
  200.1 79.8 %copy-start.50 = (f32[3072]{0:T(1024)S(1)}, f32[3072]{0:T(1024)}, u32[]{:S(2)}) copy-start(f32[3072]{0:T(1024)} %dynamic-slice_convert_fusion) | copy-start | bytes 36868
  279.9 18.1 %copy-start.22 = (bf16[768,3072]{1,0:T(8,128)(2,1)S(1)}, bf16[768,3072]{1,0:T(8,128)(2,1)}, u32[]{:S(2)}) copy-start(bf16[768,3072]{1,0:T(8,128)(2,1)} %all-gather.11.cloned.1.call-done) | copy-start | bytes 14155780
  298.0 7.4 copy-start.59
  308.9 4.5 copy-start.11
  308.9 4.7 copy-start.16
  319.7 327.9 %reduce-scatter.11.cloned.1.call-start = ((), (), s32[]{:S(2)}) async-start(), calls=%async_computation.10 | async-start | bytes 7962624 | tf_op jit(solution)/shard_map/reduce_scatter | solution.py:209
  329.3 10.3 copy-start.7
  401.2 7.1 copy-start.1
  401.2 7.1 copy-start.4
  401.2 7.3 copy-start.6
  419.4 10.1 copy-start.7
  490.3 7.1 copy-start.1
  490.3 7.1 copy-start.4
  490.3 7.3 copy-start.6
  519.5 293.0 %reduce-scatter.17.cloned.1.call-start = ((), (), s32[]{:S(2)}) async-start(), calls=%async_computation.13 | async-start | bytes 10616832 | tf_op jit(solution)/shard_map/reduce_scatter | solution.py:213
  533.8 443.5 %reduce-scatter.15.cloned.1.call-start = ((), (), s32[]{:S(2)}) async-start(), calls=%async_computation.12 | async-start | bytes 10616832 | tf_op jit(solution)/shard_map/reduce_scatter | solution.py:211
  546.2 496.3 %reduce-scatter.19.cloned.1.call-start = ((), (), s32[]{:S(2)}) async-start(), calls=%async_computation.14 | async-start | bytes 442368
  567.0 8.4 copy-start.53
  567.0 9.5 copy-start.58
  573.5 403.9 %copy-start.13 = (f32[1024,768]{0,1:T(8,128)S(1)}, f32[1024,768]{0,1:T(8,128)}, u32[]{:S(2)}) copy-start(f32[1024,768]{0,1:T(8,128)} %copy-done.10) | copy-start | bytes 9437188
  573.5 403.9 %copy-start.54 = (f32[768]{0:T(1024)S(1)}, f32[768]{0:T(1024)}, u32[]{:S(2)}) copy-start(f32[768]{0:T(1024)} %get-tuple-element.271) | copy-start | bytes 9220
  573.5 533.9 %reduce-scatter.21.cloned.1.call-start = ((), (), s32[]{:S(2)}) async-start(), calls=%async_computation.15 | async-start | bytes 442368
  576.5 607.6 %all-reduce.5.cloned.1.call-start = ((), (), s32[]{:S(2)}) async-start(), calls=%async_computation.16 | async-start | bytes 7077888 | tf_op jit(solution)/shard_map/psum | solution.py:215
  1184.0 5.0 copy-start.27
  (33 other events, 71.6 us)
Sparse Core Ops, SparseCore 0:
  10.2 67.6 all-gather.6
  80.0 39.8 all-gather.8
  122.1 78.0 all-gather.10
  202.2 77.6 all-gather.12
  319.9 67.9 reduce-scatter.12
  519.6 127.8 reduce-scatter.10
  651.2 161.2 reduce-scatter.16
  816.1 161.2 reduce-scatter.14
  981.2 61.2 reduce-scatter.18
  1046.2 61.2 reduce-scatter.20
  1110.1 73.9 all-reduce.4
